TPU v7x, 32 devices: a whole 2x2x4 slice. The times are simulated.
32 devices in a mesh: row: 8 (over y, x, core), col: 4 (over z).
Axes of the slice: x: 2, y: 2, z: 4, core: 2. Of those that a mesh axis runs over, the one named last changes fastest.
Arguments:
- query_proj: bfloat16 [192, 192, 128], P('row', 'col'), may hold values from -8 to 8
- key_proj: bfloat16 [192, 192, 128], P('row', 'col'), may hold values from -8 to 8
- value_proj: bfloat16 [192, 192, 128], P('row', 'col'), may hold values from -6 to 6
- pair_bias: bfloat16 [4, 192, 192], P(None, 'col', 'row'), may hold values from -9 to 9
- pair_mask: int32 [192, 192], P('row', 'col'), may hold values 0 or 1
- grad_out: bfloat16 [192, 192, 128], P('row', 'col'), may hold values from -18 to 18
Outputs:
- grad_query: bfloat16 [192, 192, 128], P('row', 'col')
- grad_key: bfloat16 [192, 192, 128], P('row', 'col')
- grad_value: bfloat16 [192, 192, 128], P('row', 'col')
- grad_bias: float32 [4, 192, 192], P(None, 'col', 'row')
All inputs are finite; a program needn't handle non-finite values. No bound on the sum of `pair_mask` on one device may be relied on, other than what follows from the above.
Results may differ from a plain program's by a relative error of at most 0.0096.
Values may be sent and summed in bfloat16 or wider, within the bound.
A program may use at most 128 MiB of HBM per device.

v0:
```python
import math
import jax
import jax.numpy as jnp
from jax import lax
from jax.sharding import PartitionSpec as P

HEADS = 4
HEAD_DIM = 32


def block_grads(queries, keys_all, values_all, grads, mask_all, bias_full):
    block_rows, query_count, channel_count = queries.shape
    key_count = keys_all.shape[1]
    scale = 1.0 / math.sqrt(HEAD_DIM)
    query_heads = queries.reshape(block_rows, query_count, HEADS, HEAD_DIM)
    key_heads = keys_all.reshape(block_rows, key_count, HEADS, HEAD_DIM)
    value_heads = values_all.reshape(block_rows, key_count, HEADS, HEAD_DIM)
    grad_heads = grads.reshape(block_rows, query_count, HEADS, HEAD_DIM)
    masked = 1000000000.0 * (mask_all.astype(jnp.float32) - 1.0)
    scores = (
        jnp.einsum("bjhd,bkhd->bhjk", query_heads, key_heads, preferred_element_type=jnp.float32)
        * scale
    )
    scores = scores + bias_full.astype(jnp.float32)[None] + masked[:, None, None, :]
    top_score = jnp.max(scores, axis=-1, keepdims=True)
    weights = jnp.exp(scores - top_score)
    attn_probs = weights / jnp.sum(weights, axis=-1, keepdims=True)
    attn_low = attn_probs.astype(jnp.bfloat16)
    attended = jnp.einsum(
        "bhjk,bkhd->bjhd", attn_low, value_heads, preferred_element_type=jnp.float32
    )
    row_delta = jnp.sum(grad_heads.astype(jnp.float32) * attended, axis=-1)
    grad_probs = jnp.einsum(
        "bjhd,bkhd->bhjk", grad_heads, value_heads, preferred_element_type=jnp.float32
    )
    grad_scores = attn_probs * (grad_probs - jnp.transpose(row_delta, (0, 2, 1))[..., None])
    scores_low = grad_scores.astype(jnp.bfloat16)
    grad_queries = (
        jnp.einsum("bhjk,bkhd->bjhd", scores_low, key_heads, preferred_element_type=jnp.float32)
        * scale
    )
    grad_keys = (
        jnp.einsum("bhjk,bjhd->bkhd", scores_low, query_heads, preferred_element_type=jnp.float32)
        * scale
    )
    grad_values = jnp.einsum(
        "bhjk,bjhd->bkhd", attn_low, grad_heads, preferred_element_type=jnp.float32
    )
    bias_grad = jnp.sum(grad_scores, axis=0)
    return (
        grad_queries.reshape(block_rows, query_count, channel_count),
        grad_keys.reshape(block_rows, key_count, channel_count),
        grad_values.reshape(block_rows, key_count, channel_count),
        bias_grad,
    )


def all_blocks(queries, keys_all, values_all, grads, mask_all, bias_full):
    row_count, query_count, channel_count = queries.shape
    key_count = keys_all.shape[1]
    block_rows = 1
    while (
        block_rows * 2 <= row_count
        and row_count % (block_rows * 2) == 0
        and (block_rows * query_count < 512)
    ):
        block_rows = block_rows * 2
    steps_count = row_count // block_rows

    def split_rows(array):
        return array.reshape((steps_count, block_rows) + array.shape[1:])

    def one_block(bias_sum, pieces):
        grad_queries, grad_keys, grad_values, bias_grad = block_grads(
            pieces[0], pieces[1], pieces[2], pieces[3], pieces[4], bias_full
        )
        return (bias_sum + bias_grad, (grad_queries, grad_keys, grad_values))

    start_sum = jnp.zeros((HEADS, query_count, key_count), jnp.float32)
    bias_sum, stacked = lax.scan(
        one_block,
        start_sum,
        (
            split_rows(queries),
            split_rows(keys_all),
            split_rows(values_all),
            split_rows(grads),
            split_rows(mask_all),
        ),
    )
    return (
        stacked[0].reshape(row_count, query_count, channel_count),
        stacked[1].reshape(row_count, key_count, channel_count),
        stacked[2].reshape(row_count, key_count, channel_count),
        bias_sum,
    )


def local(query_proj, key_proj, value_proj, pair_bias, pair_mask, grad_out):
    bias_rows = lax.all_gather(pair_bias, "row", axis=2, tiled=True)
    mask_low = pair_mask.astype(jnp.bfloat16)
    local_tiles = (
        lax.all_to_all(query_proj, "col", split_axis=0, concat_axis=1, tiled=True),
        lax.all_to_all(key_proj, "col", split_axis=0, concat_axis=1, tiled=True),
        lax.all_to_all(value_proj, "col", split_axis=0, concat_axis=1, tiled=True),
        lax.all_to_all(grad_out, "col", split_axis=0, concat_axis=1, tiled=True),
        lax.all_to_all(mask_low, "col", split_axis=0, concat_axis=1, tiled=True),
    )
    bias_full = lax.all_gather(bias_rows, "col", axis=1, tiled=True)
    grad_queries, grad_keys, grad_values, bias_whole = all_blocks(
        local_tiles[0], local_tiles[1], local_tiles[2], local_tiles[3], local_tiles[4], bias_full
    )
    grad_query, grad_key, grad_value = (
        lax.all_to_all(
            grad_queries.astype(jnp.bfloat16), "col", split_axis=1, concat_axis=0, tiled=True
        ),
        lax.all_to_all(
            grad_keys.astype(jnp.bfloat16), "col", split_axis=1, concat_axis=0, tiled=True
        ),
        lax.all_to_all(
            grad_values.astype(jnp.bfloat16), "col", split_axis=1, concat_axis=0, tiled=True
        ),
    )
    bias_part = lax.psum_scatter(bias_whole, "col", scatter_dimension=1, tiled=True)
    grad_bias = lax.psum_scatter(bias_part, "row", scatter_dimension=2, tiled=True)
    return (grad_query, grad_key, grad_value, grad_bias)


def solution(mesh):
    placed = (
        P("row", "col", None),
        P("row", "col", None),
        P("row", "col", None),
        P(None, "col", "row"),
        P("row", "col"),
        P("row", "col", None),
    )
    return jax.shard_map(
        local,
        mesh=mesh,
        in_specs=placed,
        out_specs=(
            P("row", "col", None),
            P("row", "col", None),
            P("row", "col", None),
            P(None, "col", "row"),
        ),
        check_vma=False,
    )
```

profile of v0, /device:TPU:0, one launch (start us, length us, event | category | flops | bytes accessed | tf_op | source)
XLA Modules:
  0.0 196.8 jit_solution(4565069296105848895)
XLA Ops:
  7.2 0.7 convert_element_type.60
  8.0 11.7 %all_to_all.130 = bf16[4,2,144]{2,1,0:T(2,128)(2,1)S(1)} all-to-all(bf16[4,2,144]{2,1,0:T(2,128)(2,1)S(1)} %reshape.104), channel_id=1, replica_groups=mesh['row'=8,'col'=4] {'col'}, dimensions={0} | all-to-all | bytes 4608 | tf_op jit(solution)/shard_map/all_to_all | solution.py:107
  19.7 11.8 %all_to_all.131 = bf16[24,48,128]{2,1,0:T(8,128)(2,1)S(1)} all-to-all(bf16[24,48,128]{2,1,0:T(8,128)(2,1)} %param.8), channel_id=1, replica_groups=mesh['row'=8,'col'=4] {'col'}, dimensions={0} | all-to-all | bytes 589824 | tf_op jit(solution)/shard_map/all_to_all | solution.py:103
  31.6 11.7 %all_to_all.132 = bf16[24,48,128]{2,1,0:T(8,128)(2,1)S(1)} all-to-all(bf16[24,48,128]{2,1,0:T(8,128)(2,1)} %param.9), channel_id=1, replica_groups=mesh['row'=8,'col'=4] {'col'}, dimensions={0} | all-to-all | bytes 589824 | tf_op jit(solution)/shard_map/all_to_all | solution.py:104
  43.3 11.6 %all_to_all.133 = bf16[24,48,128]{2,1,0:T(8,128)(2,1)S(1)} all-to-all(bf16[24,48,128]{2,1,0:T(8,128)(2,1)} %param.10), channel_id=1, replica_groups=mesh['row'=8,'col'=4] {'col'}, dimensions={0} | all-to-all | bytes 589824 | tf_op jit(solution)/shard_map/all_to_all | solution.py:105
  54.9 3.5 %all-to-all-start.3 = ((bf16[24,48,128]{2,1,0:T(8,128)(2,1)}), bf16[24,48,128]{2,1,0:T(8,128)(2,1)S(1)}, u32[]{:S(2)}, u32[]{:S(2)}) async-start(bf16[24,48,128]{2,1,0:T(8,128)(2,1)} %param.13), calls=%async_computation.3 | async-start | bytes 589824 | tf_op jit(solution)/shard_map/all_to_all | solution.py:106
  58.5 9.3 %all_gather.6 = bf16[4,48,192]{1,0,2:T(4,128)(2,1)S(1)} all-gather(bf16[4,48,24]{1,0,2:T(4,128)(2,1)S(1)} %copy.115), channel_id=1, replica_groups=mesh['row'=8,'col'=4] {'row'}, dimensions={2}, use_global_device_ids=true | all-gather | bytes 82944 | tf_op jit(solution)/shard_map/all_gather | solution.py:100
  67.9 15.1 %all_gather.7 = bf16[4,192,192]{2,0,1:T(4,128)(2,1)S(1)} all-gather(bf16[4,48,192]{2,0,1:T(4,128)(2,1)S(1)} %copy.116), channel_id=1, replica_groups=mesh['row'=8,'col'=4] {'col'}, dimensions={1}, use_global_device_ids=true | all-gather | bytes 368640 | tf_op jit(solution)/shard_map/all_gather | solution.py:109
  83.6 0.7 copy.113
  84.4 23.5 %while.19 = (s32[]{:T(128)}, f32[4,192,192]{1,2,0:T(8,128)S(1)}, bf16[3,2,192,128]{3,2,1,0:T(8,128)(2,1)}, bf16[3,2,192,128]{3,2,1,0:T(8,128)(2,1)}, bf16[3,2,19...) while((s32[]{:T(128)}, f32[4,192,192]{1,2,0:T(8,128)S(1)}, ...), condition=%wide.region_5.6_spmd.clone, body=%wide.region_0.5_spmd.clone.sunk | while | flops 117423936 | bytes 24709288 | solution.py:80
  84.5 0.9 copy.164
  85.7 0.9 constant_dynamic-slice_fusion.10
  86.8 0.8 fusion.54
  87.8 0.7 copy-done.2
  89.2 0.5 fusion.57
  90.9 0.7 constant_dynamic-update-slice_fusion.5
  91.5 0.7 constant_dynamic-update-slice_fusion.6
  92.3 0.9 copy.164
  93.5 0.9 constant_dynamic-slice_fusion.10
  94.7 0.8 fusion.54
  95.6 0.7 copy-done.2
  97.1 0.5 fusion.57
  98.7 0.7 constant_dynamic-update-slice_fusion.5
  99.4 0.7 constant_dynamic-update-slice_fusion.6
  100.2 0.9 copy.164
  101.4 0.9 constant_dynamic-slice_fusion.10
  102.5 0.8 fusion.54
  103.4 0.7 copy-done.2
  104.9 0.5 fusion.57
  106.5 0.7 constant_dynamic-update-slice_fusion.5
  107.2 0.7 constant_dynamic-update-slice_fusion.6
  107.9 0.4 copy.145
  108.3 1.3 reshape.102
  109.6 1.9 copy.134
  111.5 5.4 %all-to-all-start.7 = ((bf16[6,192,128]{2,0,1:T(8,128)(2,1)}), bf16[6,192,128]{2,0,1:T(8,128)(2,1)S(1)}, u32[]{:S(2)}, u32[]{:S(2)}) async-start(bf16[6,192,128]{2,0,1:T(8,128)(2,1)} %copy.134), calls=%async_computation.7 | async-start | bytes 786432 | tf_op jit(solution)/shard_map/all_to_all | solution.py:120
  116.9 1.0 copy.126
  117.9 17.4 %all-to-all-done.7 = bf16[6,192,128]{2,0,1:T(8,128)(2,1)S(1)} async-done(((bf16[6,192,128]{2,0,1:T(8,128)(2,1)}), bf16[6,192,128]{2,0,1:T(8,128)(2,1)S(1)}, u32[]{:S(2)}, u32[]{:S(2)}) %all-to-all-start.7) | async-done | bytes 294944 | tf_op jit(solution)/shard_map/all_to_all | solution.py:120
  135.3 3.5 %all-to-all-start.5 = ((bf16[6,192,128]{2,0,1:T(8,128)(2,1)}), bf16[6,192,128]{2,0,1:T(8,128)(2,1)S(1)}, u32[]{:S(2)}, u32[]{:S(2)}) async-start(bf16[6,192,128]{2,0,1:T(8,128)(2,1)} %copy.126), calls=%async_computation.5 | async-start | bytes 786432 | tf_op jit(solution)/shard_map/all_to_all | solution.py:114
  138.8 1.9 copy.130
  140.7 6.9 %all-to-all-done.5 = bf16[6,192,128]{2,0,1:T(8,128)(2,1)S(1)} async-done(((bf16[6,192,128]{2,0,1:T(8,128)(2,1)}), bf16[6,192,128]{2,0,1:T(8,128)(2,1)S(1)}, u32[]{:S(2)}, u32[]{:S(2)}) %all-to-all-start.5) | async-done | bytes 294944 | tf_op jit(solution)/shard_map/all_to_all | solution.py:114
  147.6 3.5 %all-to-all-start.6 = ((bf16[6,192,128]{2,0,1:T(8,128)(2,1)}), bf16[6,192,128]{2,0,1:T(8,128)(2,1)S(1)}, u32[]{:S(2)}, u32[]{:S(2)}) async-start(bf16[6,192,128]{2,0,1:T(8,128)(2,1)} %copy.130), calls=%async_computation.6 | async-start | bytes 786432 | tf_op jit(solution)/shard_map/all_to_all | solution.py:117
  151.2 1.1 reshape.103
  152.2 0.9 copy.146
  153.2 0.8 copy.136
  154.0 0.8 copy.128
  154.7 5.2 %all-to-all-done.6 = bf16[6,192,128]{2,0,1:T(8,128)(2,1)S(1)} async-done(((bf16[6,192,128]{2,0,1:T(8,128)(2,1)}), bf16[6,192,128]{2,0,1:T(8,128)(2,1)S(1)}, u32[]{:S(2)}, u32[]{:S(2)}) %all-to-all-start.6) | async-done | bytes 294944 | tf_op jit(solution)/shard_map/all_to_all | solution.py:117
  160.0 0.8 copy.132
  160.7 29.2 %reduce-scatter.5.cloned.1.call-done = f32[4,48,24]{1,2,0:T(8,128)} async-done(((f32[4,48,192]{1,2,0:T(8,128)}), f32[4,48,24]{1,2,0:T(8,128)}) %reduce-scatter.5.cloned.1.call-update) | async-done | bytes 18448 | tf_op jit(solution)/shard_map/reduce_scatter | solution.py:125
  (127 shorter events, 8.3 us)
Async XLA Ops:
  7.2 51.3 %copy-start.10 = (bf16[4,48,24]{1,2,0:T(8,128)(2,1)S(1)}, bf16[4,48,24]{1,2,0:T(8,128)(2,1)}, u32[]{:S(2)}) copy-start(bf16[4,48,24]{1,2,0:T(8,128)(2,1)} %param.11) | copy-start | bytes 27652
  54.9 29.4 %all-to-all-start.3 = ((bf16[24,48,128]{2,1,0:T(8,128)(2,1)}), bf16[24,48,128]{2,1,0:T(8,128)(2,1)S(1)}, u32[]{:S(2)}, u32[]{:S(2)}) async-start(bf16[24,48,128]{2,1,0:T(8,128)(2,1)} %param.13), calls=%async_computation.3 | async-start | bytes 589824 | tf_op jit(solution)/shard_map/all_to_all | solution.py:106
  58.4 92.8 %reduce-scatter.7.cloned.1.call-start = ((), (), s32[]{:S(2)}) async-start(), calls=%async_computation.11 | async-start | bytes 737280
  84.4 2.3 %copy-start = (bf16[4,192,192]{1,2,0:T(8,128)(2,1)}, bf16[4,192,192]{1,2,0:T(8,128)(2,1)S(1)}, u32[]{:S(2)}) copy-start(bf16[4,192,192]{1,2,0:T(8,128)(2,1)S(1)} %get-tuple-element.381) | copy-start | bytes 884740 | tf_op jit(solution)/shard_map/while
  84.4 2.3 %copy-start.3 = (bf16[3,2,192,128]{3,2,1,0:T(8,128)(2,1)}, bf16[3,2,192,128]{3,2,1,0:T(8,128)(2,1)S(1)}, u32[]{:S(2)}) copy-start(bf16[3,2,192,128]{3,2,1,0:T(8,128)(2,1)S(1)} %get-tuple-element.380) | copy-start | bytes 884740 | tf_op jit(solution)/shard_map/while
  84.4 2.3 %copy-start.5 = (bf16[3,2,192,128]{3,2,1,0:T(8,128)(2,1)}, bf16[3,2,192,128]{3,2,1,0:T(8,128)(2,1)S(1)}, u32[]{:S(2)}) copy-start(bf16[3,2,192,128]{3,2,1,0:T(8,128)(2,1)S(1)} %get-tuple-element.384) | copy-start | bytes 884740 | tf_op jit(solution)/shard_map/while
  84.4 2.3 %copy-start.7 = (bf16[3,2,192,128]{3,2,1,0:T(8,128)(2,1)}, bf16[3,2,192,128]{3,2,1,0:T(8,128)(2,1)S(1)}, u32[]{:S(2)}) copy-start(bf16[3,2,192,128]{3,2,1,0:T(8,128)(2,1)S(1)} %get-tuple-element.383) | copy-start | bytes 884740 | tf_op jit(solution)/shard_map/while
  87.6 0.9 copy-start.2
  90.0 2.2 %copy-start.1 = (bf16[4,192,192]{1,2,0:T(8,128)(2,1)S(1)}, bf16[4,192,192]{1,2,0:T(8,128)(2,1)}, u32[]{:S(2)}) copy-start(bf16[4,192,192]{1,2,0:T(8,128)(2,1)} %copy-done) | copy-start | bytes 884740 | tf_op jit(solution)/shard_map/while
  90.0 2.2 %copy-start.4 = (bf16[3,2,192,128]{3,2,1,0:T(8,128)(2,1)S(1)}, bf16[3,2,192,128]{3,2,1,0:T(8,128)(2,1)}, u32[]{:S(2)}) copy-start(bf16[3,2,192,128]{3,2,1,0:T(8,128)(2,1)} %copy-done.3) | copy-start | bytes 884740 | tf_op jit(solution)/shard_map/while
  90.0 2.2 %copy-start.6 = (bf16[3,2,192,128]{3,2,1,0:T(8,128)(2,1)S(1)}, bf16[3,2,192,128]{3,2,1,0:T(8,128)(2,1)}, u32[]{:S(2)}) copy-start(bf16[3,2,192,128]{3,2,1,0:T(8,128)(2,1)} %copy-done.5) | copy-start | bytes 884740 | tf_op jit(solution)/shard_map/while
  90.0 2.2 %copy-start.8 = (bf16[3,2,192,128]{3,2,1,0:T(8,128)(2,1)S(1)}, bf16[3,2,192,128]{3,2,1,0:T(8,128)(2,1)}, u32[]{:S(2)}) copy-start(bf16[3,2,192,128]{3,2,1,0:T(8,128)(2,1)} %copy-done.7) | copy-start | bytes 884740 | tf_op jit(solution)/shard_map/while
  92.2 2.3 %copy-start = (bf16[4,192,192]{1,2,0:T(8,128)(2,1)}, bf16[4,192,192]{1,2,0:T(8,128)(2,1)S(1)}, u32[]{:S(2)}) copy-start(bf16[4,192,192]{1,2,0:T(8,128)(2,1)S(1)} %get-tuple-element.381) | copy-start | bytes 884740 | tf_op jit(solution)/shard_map/while
  92.3 2.3 %copy-start.3 = (bf16[3,2,192,128]{3,2,1,0:T(8,128)(2,1)}, bf16[3,2,192,128]{3,2,1,0:T(8,128)(2,1)S(1)}, u32[]{:S(2)}) copy-start(bf16[3,2,192,128]{3,2,1,0:T(8,128)(2,1)S(1)} %get-tuple-element.380) | copy-start | bytes 884740 | tf_op jit(solution)/shard_map/while
  92.3 2.3 %copy-start.5 = (bf16[3,2,192,128]{3,2,1,0:T(8,128)(2,1)}, bf16[3,2,192,128]{3,2,1,0:T(8,128)(2,1)S(1)}, u32[]{:S(2)}) copy-start(bf16[3,2,192,128]{3,2,1,0:T(8,128)(2,1)S(1)} %get-tuple-element.384) | copy-start | bytes 884740 | tf_op jit(solution)/shard_map/while
  92.3 2.3 %copy-start.7 = (bf16[3,2,192,128]{3,2,1,0:T(8,128)(2,1)}, bf16[3,2,192,128]{3,2,1,0:T(8,128)(2,1)S(1)}, u32[]{:S(2)}) copy-start(bf16[3,2,192,128]{3,2,1,0:T(8,128)(2,1)S(1)} %get-tuple-element.383) | copy-start | bytes 884740 | tf_op jit(solution)/shard_map/while
  95.4 0.9 copy-start.2
  97.8 2.2 %copy-start.1 = (bf16[4,192,192]{1,2,0:T(8,128)(2,1)S(1)}, bf16[4,192,192]{1,2,0:T(8,128)(2,1)}, u32[]{:S(2)}) copy-start(bf16[4,192,192]{1,2,0:T(8,128)(2,1)} %copy-done) | copy-start | bytes 884740 | tf_op jit(solution)/shard_map/while
  97.8 2.2 %copy-start.4 = (bf16[3,2,192,128]{3,2,1,0:T(8,128)(2,1)S(1)}, bf16[3,2,192,128]{3,2,1,0:T(8,128)(2,1)}, u32[]{:S(2)}) copy-start(bf16[3,2,192,128]{3,2,1,0:T(8,128)(2,1)} %copy-done.3) | copy-start | bytes 884740 | tf_op jit(solution)/shard_map/while
  97.8 2.2 %copy-start.6 = (bf16[3,2,192,128]{3,2,1,0:T(8,128)(2,1)S(1)}, bf16[3,2,192,128]{3,2,1,0:T(8,128)(2,1)}, u32[]{:S(2)}) copy-start(bf16[3,2,192,128]{3,2,1,0:T(8,128)(2,1)} %copy-done.5) | copy-start | bytes 884740 | tf_op jit(solution)/shard_map/while
  97.8 2.2 %copy-start.8 = (bf16[3,2,192,128]{3,2,1,0:T(8,128)(2,1)S(1)}, bf16[3,2,192,128]{3,2,1,0:T(8,128)(2,1)}, u32[]{:S(2)}) copy-start(bf16[3,2,192,128]{3,2,1,0:T(8,128)(2,1)} %copy-done.7) | copy-start | bytes 884740 | tf_op jit(solution)/shard_map/while
  100.1 2.3 %copy-start = (bf16[4,192,192]{1,2,0:T(8,128)(2,1)}, bf16[4,192,192]{1,2,0:T(8,128)(2,1)S(1)}, u32[]{:S(2)}) copy-start(bf16[4,192,192]{1,2,0:T(8,128)(2,1)S(1)} %get-tuple-element.381) | copy-start | bytes 884740 | tf_op jit(solution)/shard_map/while
  100.1 2.3 %copy-start.3 = (bf16[3,2,192,128]{3,2,1,0:T(8,128)(2,1)}, bf16[3,2,192,128]{3,2,1,0:T(8,128)(2,1)S(1)}, u32[]{:S(2)}) copy-start(bf16[3,2,192,128]{3,2,1,0:T(8,128)(2,1)S(1)} %get-tuple-element.380) | copy-start | bytes 884740 | tf_op jit(solution)/shard_map/while
  100.1 2.3 %copy-start.5 = (bf16[3,2,192,128]{3,2,1,0:T(8,128)(2,1)}, bf16[3,2,192,128]{3,2,1,0:T(8,128)(2,1)S(1)}, u32[]{:S(2)}) copy-start(bf16[3,2,192,128]{3,2,1,0:T(8,128)(2,1)S(1)} %get-tuple-element.384) | copy-start | bytes 884740 | tf_op jit(solution)/shard_map/while
  100.1 2.3 %copy-start.7 = (bf16[3,2,192,128]{3,2,1,0:T(8,128)(2,1)}, bf16[3,2,192,128]{3,2,1,0:T(8,128)(2,1)S(1)}, u32[]{:S(2)}) copy-start(bf16[3,2,192,128]{3,2,1,0:T(8,128)(2,1)S(1)} %get-tuple-element.383) | copy-start | bytes 884740 | tf_op jit(solution)/shard_map/while
  103.3 0.9 copy-start.2
  105.6 2.2 %copy-start.1 = (bf16[4,192,192]{1,2,0:T(8,128)(2,1)S(1)}, bf16[4,192,192]{1,2,0:T(8,128)(2,1)}, u32[]{:S(2)}) copy-start(bf16[4,192,192]{1,2,0:T(8,128)(2,1)} %copy-done) | copy-start | bytes 884740 | tf_op jit(solution)/shard_map/while
  105.7 2.2 %copy-start.4 = (bf16[3,2,192,128]{3,2,1,0:T(8,128)(2,1)S(1)}, bf16[3,2,192,128]{3,2,1,0:T(8,128)(2,1)}, u32[]{:S(2)}) copy-start(bf16[3,2,192,128]{3,2,1,0:T(8,128)(2,1)} %copy-done.3) | copy-start | bytes 884740 | tf_op jit(solution)/shard_map/while
  105.7 2.2 %copy-start.6 = (bf16[3,2,192,128]{3,2,1,0:T(8,128)(2,1)S(1)}, bf16[3,2,192,128]{3,2,1,0:T(8,128)(2,1)}, u32[]{:S(2)}) copy-start(bf16[3,2,192,128]{3,2,1,0:T(8,128)(2,1)} %copy-done.5) | copy-start | bytes 884740 | tf_op jit(solution)/shard_map/while
  105.7 2.2 %copy-start.8 = (bf16[3,2,192,128]{3,2,1,0:T(8,128)(2,1)S(1)}, bf16[3,2,192,128]{3,2,1,0:T(8,128)(2,1)}, u32[]{:S(2)}) copy-start(bf16[3,2,192,128]{3,2,1,0:T(8,128)(2,1)} %copy-done.7) | copy-start | bytes 884740 | tf_op jit(solution)/shard_map/while
  108.3 8.6 %copy-start.9 = (bf16[3,2,192,128]{3,2,1,0:T(8,128)(2,1)S(1)}, bf16[3,2,192,128]{3,2,1,0:T(8,128)(2,1)}, u32[]{:S(2)}) copy-start(bf16[3,2,192,128]{3,2,1,0:T(8,128)(2,1)} %get-tuple-element.144) | copy-start | bytes 884740
  111.5 23.8 %all-to-all-start.7 = ((bf16[6,192,128]{2,0,1:T(8,128)(2,1)}), bf16[6,192,128]{2,0,1:T(8,128)(2,1)S(1)}, u32[]{:S(2)}, u32[]{:S(2)}) async-start(bf16[6,192,128]{2,0,1:T(8,128)(2,1)} %copy.134), calls=%async_computation.7 | async-start | bytes 786432 | tf_op jit(solution)/shard_map/all_to_all | solution.py:120
  135.3 12.3 %all-to-all-start.5 = ((bf16[6,192,128]{2,0,1:T(8,128)(2,1)}), bf16[6,192,128]{2,0,1:T(8,128)(2,1)S(1)}, u32[]{:S(2)}, u32[]{:S(2)}) async-start(bf16[6,192,128]{2,0,1:T(8,128)(2,1)} %copy.126), calls=%async_computation.5 | async-start | bytes 786432 | tf_op jit(solution)/shard_map/all_to_all | solution.py:114
  147.6 12.3 %all-to-all-start.6 = ((bf16[6,192,128]{2,0,1:T(8,128)(2,1)}), bf16[6,192,128]{2,0,1:T(8,128)(2,1)S(1)}, u32[]{:S(2)}, u32[]{:S(2)}) async-start(bf16[6,192,128]{2,0,1:T(8,128)(2,1)} %copy.130), calls=%async_computation.6 | async-start | bytes 786432 | tf_op jit(solution)/shard_map/all_to_all | solution.py:117
  151.1 38.8 %reduce-scatter.5.cloned.1.call-start = ((), (), s32[]{:S(2)}) async-start(), calls=%async_computation.10 | async-start | bytes 442368 | tf_op jit(solution)/shard_map/reduce_scatter | solution.py:125
Sparse Core Ops, SparseCore 0:
  109.7 25.3 reduce-scatter.6
  155.6 34.3 reduce-scatter.4
where the time goes:
time: 198 us; the launch traced here: 197 us
  blocking collectives  71.3 us (36%)
  waiting for transfers between devices  58.9 us (30%)
  local copies, waits for them, and re-layouts  26.4 us (13%)
  starting transfers between devices  15.8 us (8%)
  between operations  14.2 us (7%)
  matrix products  7.33 us (4%)
  other arithmetic  2.1 us (1%)
    reduce_scatter x1, waiting for transfers between devices, local(): lax.psum_scatter(bias_part, 'row', scatter_dimension=2, tiled=True)  29.2 us
    all_to_all x1, waiting for transfers between devices, local(): lax.all_to_all(grad_values.astype(jnp.bfloat16), 'col', split_axis=1, con...  17.4 us
    all_gather x1, blocking collectives, local(): bias_full = lax.all_gather(bias_rows, 'col', axis=1, tiled=True)  15.1 us
    all_to_all x1, blocking collectives, local(): lax.all_to_all(query_proj, 'col', split_axis=0, concat_axis=1, tiled=True)  11.8 us
    all_to_all x1, blocking collectives, local(): lax.all_to_all(key_proj, 'col', split_axis=0, concat_axis=1, tiled=True)  11.7 us
    all_to_all x1, blocking collectives, local(): lax.all_to_all(mask_low, 'col', split_axis=0, concat_axis=1, tiled=True)  11.7 us
    all_to_all x1, blocking collectives, local(): lax.all_to_all(value_proj, 'col', split_axis=0, concat_axis=1, tiled=True)  11.6 us
    all_gather x1, blocking collectives, local(): bias_rows = lax.all_gather(pair_bias, 'row', axis=2, tiled=True)  9.27 us
  transfers between devices with their start and end apart: 6, of which 4 were waited for; matrix products, arithmetic and copies ran while one was open for 5% of the time, Pallas kernels for 0%

commit v1 on v0

--- a/solution.py
+++ b/solution.py
@@ -104,7 +104,12 @@
         lax.all_to_all(key_proj, "col", split_axis=0, concat_axis=1, tiled=True),
         lax.all_to_all(value_proj, "col", split_axis=0, concat_axis=1, tiled=True),
         lax.all_to_all(grad_out, "col", split_axis=0, concat_axis=1, tiled=True),
-        lax.all_to_all(mask_low, "col", split_axis=0, concat_axis=1, tiled=True),
+        jnp.concatenate(
+            lax.all_to_all(
+                jnp.stack(jnp.split(mask_low, lax.axis_size("col"), axis=0)), "col", 0, 0
+            ),
+            axis=1,
+        ),
     )
     bias_full = lax.all_gather(bias_rows, "col", axis=1, tiled=True)
     grad_queries, grad_keys, grad_values, bias_whole = all_blocks(

time: 198 us -> 198 us (level)
  no operation moved by 1% of the time
where the time goes in v1:
time: 198 us; the launch traced here: 197 us
  blocking collectives  71.3 us (36%)
  waiting for transfers between devices  58.9 us (30%)
  local copies, waits for them, and re-layouts  26.5 us (13%)
  starting transfers between devices  15.8 us (8%)
  between operations  14.2 us (7%)
  matrix products  7.32 us (4%)
  other arithmetic  2.11 us (1%)
    reduce_scatter x1, waiting for transfers between devices, local(): lax.psum_scatter(bias_part, 'row', scatter_dimension=2, tiled=True)  29.2 us
    all_to_all x1, waiting for transfers between devices, local(): lax.all_to_all(grad_values.astype(jnp.bfloat16), 'col', split_axis=1, con...  17.4 us
    all_gather x1, blocking collectives, local(): bias_full = lax.all_gather(bias_rows, 'col', axis=1, tiled=True)  15.1 us
    all_to_all x1, blocking collectives, local(): lax.all_to_all(query_proj, 'col', split_axis=0, concat_axis=1, tiled=True)  11.8 us
    all_to_all x1, blocking collectives, local(): lax.all_to_all(key_proj, 'col', split_axis=0, concat_axis=1, tiled=True)  11.7 us
    all_to_all x1, blocking collectives, local(): lax.all_to_all(jnp.stack(jnp.split(mask_low, lax.axis_size('col'), axis=0...  11.7 us
    all_to_all x1, blocking collectives, local(): lax.all_to_all(value_proj, 'col', split_axis=0, concat_axis=1, tiled=True)  11.6 us
    all_gather x1, blocking collectives, local(): bias_rows = lax.all_gather(pair_bias, 'row', axis=2, tiled=True)  9.27 us
  transfers between devices with their start and end apart: 6, of which 4 were waited for; matrix products, arithmetic and copies ran while one was open for 5% of the time, Pallas kernels for 0%

profile of v1, /device:TPU:0, one launch (start us, length us, event | category | flops | bytes accessed | tf_op | source)
XLA Modules:
  0.0 196.9 jit_solution(5455818766581730597)
XLA Ops:
  7.2 0.7 convert_element_type.60
  8.0 11.7 %all_to_all.119 = bf16[4,2,144]{2,1,0:T(2,128)(2,1)S(1)} all-to-all(bf16[4,2,144]{2,1,0:T(2,128)(2,1)S(1)} %reshape.100), channel_id=1, replica_groups=mesh['row'=8,'col'=4] {'col'}, dimensions={0} | all-to-all | bytes 4608 | tf_op jit(solution)/shard_map/all_to_all | solution.py:108
  19.7 11.8 %all_to_all.120 = bf16[24,48,128]{2,1,0:T(8,128)(2,1)S(1)} all-to-all(bf16[24,48,128]{2,1,0:T(8,128)(2,1)} %param.8), channel_id=1, replica_groups=mesh['row'=8,'col'=4] {'col'}, dimensions={0} | all-to-all | bytes 589824 | tf_op jit(solution)/shard_map/all_to_all | solution.py:103
  31.6 11.7 %all_to_all.121 = bf16[24,48,128]{2,1,0:T(8,128)(2,1)S(1)} all-to-all(bf16[24,48,128]{2,1,0:T(8,128)(2,1)} %param.9), channel_id=1, replica_groups=mesh['row'=8,'col'=4] {'col'}, dimensions={0} | all-to-all | bytes 589824 | tf_op jit(solution)/shard_map/all_to_all | solution.py:104
  43.3 11.6 %all_to_all.122 = bf16[24,48,128]{2,1,0:T(8,128)(2,1)S(1)} all-to-all(bf16[24,48,128]{2,1,0:T(8,128)(2,1)} %param.10), channel_id=1, replica_groups=mesh['row'=8,'col'=4] {'col'}, dimensions={0} | all-to-all | bytes 589824 | tf_op jit(solution)/shard_map/all_to_all | solution.py:105
  54.9 3.5 %all-to-all-start.3 = ((bf16[24,48,128]{2,1,0:T(8,128)(2,1)}), bf16[24,48,128]{2,1,0:T(8,128)(2,1)S(1)}, u32[]{:S(2)}, u32[]{:S(2)}) async-start(bf16[24,48,128]{2,1,0:T(8,128)(2,1)} %param.13), calls=%async_computation.3 | async-start | bytes 589824 | tf_op jit(solution)/shard_map/all_to_all | solution.py:106
  58.5 9.3 %all_gather.6 = bf16[4,48,192]{1,0,2:T(4,128)(2,1)S(1)} all-gather(bf16[4,48,24]{1,0,2:T(4,128)(2,1)S(1)} %copy.116), channel_id=1, replica_groups=mesh['row'=8,'col'=4] {'row'}, dimensions={2}, use_global_device_ids=true | all-gather | bytes 82944 | tf_op jit(solution)/shard_map/all_gather | solution.py:100
  68.0 15.1 %all_gather.7 = bf16[4,192,192]{2,0,1:T(4,128)(2,1)S(1)} all-gather(bf16[4,48,192]{2,0,1:T(4,128)(2,1)S(1)} %copy.117), channel_id=1, replica_groups=mesh['row'=8,'col'=4] {'col'}, dimensions={1}, use_global_device_ids=true | all-gather | bytes 368640 | tf_op jit(solution)/shard_map/all_gather | solution.py:114
  83.6 0.8 copy.114
  84.4 23.6 %while.19 = (s32[]{:T(128)}, f32[4,192,192]{1,2,0:T(8,128)S(1)}, bf16[3,2,192,128]{3,2,1,0:T(8,128)(2,1)}, bf16[3,2,192,128]{3,2,1,0:T(8,128)(2,1)}, bf16[3,2,19...) while((s32[]{:T(128)}, f32[4,192,192]{1,2,0:T(8,128)S(1)}, ...), condition=%wide.region_5.6_spmd.clone, body=%wide.region_0.5_spmd.clone.sunk | while | flops 117423936 | bytes 24709288 | solution.py:80
  84.5 1.0 copy.165
  85.7 0.9 constant_dynamic-slice_fusion.10
  86.9 0.8 fusion.54
  87.8 0.7 copy-done.2
  89.3 0.5 fusion.57
  90.9 0.7 constant_dynamic-update-slice_fusion.5
  91.6 0.7 constant_dynamic-update-slice_fusion.6
  92.4 1.0 copy.165
  93.6 0.9 constant_dynamic-slice_fusion.10
  94.7 0.8 fusion.54
  95.7 0.7 copy-done.2
  97.1 0.5 fusion.57
  98.8 0.7 constant_dynamic-update-slice_fusion.5
  99.4 0.7 constant_dynamic-update-slice_fusion.6
  100.2 1.0 copy.165
  101.4 0.9 constant_dynamic-slice_fusion.10
  102.6 0.8 fusion.54
  103.5 0.7 copy-done.2
  105.0 0.5 fusion.57
  106.6 0.7 constant_dynamic-update-slice_fusion.5
  107.3 0.7 constant_dynamic-update-slice_fusion.6
  108.0 0.4 copy.146
  108.4 1.3 reshape.98
  109.7 1.9 copy.135
  111.6 5.4 %all-to-all-start.7 = ((bf16[6,192,128]{2,0,1:T(8,128)(2,1)}), bf16[6,192,128]{2,0,1:T(8,128)(2,1)S(1)}, u32[]{:S(2)}, u32[]{:S(2)}) async-start(bf16[6,192,128]{2,0,1:T(8,128)(2,1)} %copy.135), calls=%async_computation.7 | async-start | bytes 786432 | tf_op jit(solution)/shard_map/all_to_all | solution.py:125
  117.0 1.0 copy.127
  118.0 17.4 %all-to-all-done.7 = bf16[6,192,128]{2,0,1:T(8,128)(2,1)S(1)} async-done(((bf16[6,192,128]{2,0,1:T(8,128)(2,1)}), bf16[6,192,128]{2,0,1:T(8,128)(2,1)S(1)}, u32[]{:S(2)}, u32[]{:S(2)}) %all-to-all-start.7) | async-done | bytes 294944 | tf_op jit(solution)/shard_map/all_to_all | solution.py:125
  135.4 3.5 %all-to-all-start.5 = ((bf16[6,192,128]{2,0,1:T(8,128)(2,1)}), bf16[6,192,128]{2,0,1:T(8,128)(2,1)S(1)}, u32[]{:S(2)}, u32[]{:S(2)}) async-start(bf16[6,192,128]{2,0,1:T(8,128)(2,1)} %copy.127), calls=%async_computation.5 | async-start | bytes 786432 | tf_op jit(solution)/shard_map/all_to_all | solution.py:119
  138.9 1.9 copy.131
  140.8 6.9 %all-to-all-done.5 = bf16[6,192,128]{2,0,1:T(8,128)(2,1)S(1)} async-done(((bf16[6,192,128]{2,0,1:T(8,128)(2,1)}), bf16[6,192,128]{2,0,1:T(8,128)(2,1)S(1)}, u32[]{:S(2)}, u32[]{:S(2)}) %all-to-all-start.5) | async-done | bytes 294944 | tf_op jit(solution)/shard_map/all_to_all | solution.py:119
  147.7 3.5 %all-to-all-start.6 = ((bf16[6,192,128]{2,0,1:T(8,128)(2,1)}), bf16[6,192,128]{2,0,1:T(8,128)(2,1)S(1)}, u32[]{:S(2)}, u32[]{:S(2)}) async-start(bf16[6,192,128]{2,0,1:T(8,128)(2,1)} %copy.131), calls=%async_computation.6 | async-start | bytes 786432 | tf_op jit(solution)/shard_map/all_to_all | solution.py:122
  151.3 1.1 reshape.99
  152.3 0.9 copy.147
  153.3 0.8 copy.137
  154.1 0.8 copy.129
  154.8 5.2 %all-to-all-done.6 = bf16[6,192,128]{2,0,1:T(8,128)(2,1)S(1)} async-done(((bf16[6,192,128]{2,0,1:T(8,128)(2,1)}), bf16[6,192,128]{2,0,1:T(8,128)(2,1)S(1)}, u32[]{:S(2)}, u32[]{:S(2)}) %all-to-all-start.6) | async-done | bytes 294944 | tf_op jit(solution)/shard_map/all_to_all | solution.py:122
  160.0 0.8 copy.133
  160.8 29.2 %reduce-scatter.5.cloned.1.call-done = f32[4,48,24]{1,2,0:T(8,128)} async-done(((f32[4,48,192]{1,2,0:T(8,128)}), f32[4,48,24]{1,2,0:T(8,128)}) %reduce-scatter.5.cloned.1.call-update) | async-done | bytes 18448 | tf_op jit(solution)/shard_map/reduce_scatter | solution.py:130
  (128 shorter events, 8.3 us)
Async XLA Ops:
  7.2 51.3 %copy-start.10 = (bf16[4,48,24]{1,2,0:T(8,128)(2,1)S(1)}, bf16[4,48,24]{1,2,0:T(8,128)(2,1)}, u32[]{:S(2)}) copy-start(bf16[4,48,24]{1,2,0:T(8,128)(2,1)} %param.11) | copy-start | bytes 27652
  54.9 29.4 %all-to-all-start.3 = ((bf16[24,48,128]{2,1,0:T(8,128)(2,1)}), bf16[24,48,128]{2,1,0:T(8,128)(2,1)S(1)}, u32[]{:S(2)}, u32[]{:S(2)}) async-start(bf16[24,48,128]{2,1,0:T(8,128)(2,1)} %param.13), calls=%async_computation.3 | async-start | bytes 589824 | tf_op jit(solution)/shard_map/all_to_all | solution.py:106
  58.4 92.9 %reduce-scatter.7.cloned.1.call-start = ((), (), s32[]{:S(2)}) async-start(), calls=%async_computation.11 | async-start | bytes 737280
  84.4 2.3 %copy-start = (bf16[4,192,192]{1,2,0:T(8,128)(2,1)}, bf16[4,192,192]{1,2,0:T(8,128)(2,1)S(1)}, u32[]{:S(2)}) copy-start(bf16[4,192,192]{1,2,0:T(8,128)(2,1)S(1)} %get-tuple-element.385) | copy-start | bytes 884740 | tf_op jit(solution)/shard_map/while
  84.4 2.3 %copy-start.3 = (bf16[3,2,192,128]{3,2,1,0:T(8,128)(2,1)}, bf16[3,2,192,128]{3,2,1,0:T(8,128)(2,1)S(1)}, u32[]{:S(2)}) copy-start(bf16[3,2,192,128]{3,2,1,0:T(8,128)(2,1)S(1)} %get-tuple-element.384) | copy-start | bytes 884740 | tf_op jit(solution)/shard_map/while
  84.5 2.3 %copy-start.5 = (bf16[3,2,192,128]{3,2,1,0:T(8,128)(2,1)}, bf16[3,2,192,128]{3,2,1,0:T(8,128)(2,1)S(1)}, u32[]{:S(2)}) copy-start(bf16[3,2,192,128]{3,2,1,0:T(8,128)(2,1)S(1)} %get-tuple-element.388) | copy-start | bytes 884740 | tf_op jit(solution)/shard_map/while
  84.5 2.3 %copy-start.7 = (bf16[3,2,192,128]{3,2,1,0:T(8,128)(2,1)}, bf16[3,2,192,128]{3,2,1,0:T(8,128)(2,1)S(1)}, u32[]{:S(2)}) copy-start(bf16[3,2,192,128]{3,2,1,0:T(8,128)(2,1)S(1)} %get-tuple-element.387) | copy-start | bytes 884740 | tf_op jit(solution)/shard_map/while
  87.6 0.9 copy-start.2
  90.0 2.2 %copy-start.1 = (bf16[4,192,192]{1,2,0:T(8,128)(2,1)S(1)}, bf16[4,192,192]{1,2,0:T(8,128)(2,1)}, u32[]{:S(2)}) copy-start(bf16[4,192,192]{1,2,0:T(8,128)(2,1)} %copy-done) | copy-start | bytes 884740 | tf_op jit(solution)/shard_map/while
  90.0 2.2 %copy-start.4 = (bf16[3,2,192,128]{3,2,1,0:T(8,128)(2,1)S(1)}, bf16[3,2,192,128]{3,2,1,0:T(8,128)(2,1)}, u32[]{:S(2)}) copy-start(bf16[3,2,192,128]{3,2,1,0:T(8,128)(2,1)} %copy-done.3) | copy-start | bytes 884740 | tf_op jit(solution)/shard_map/while
  90.0 2.2 %copy-start.6 = (bf16[3,2,192,128]{3,2,1,0:T(8,128)(2,1)S(1)}, bf16[3,2,192,128]{3,2,1,0:T(8,128)(2,1)}, u32[]{:S(2)}) copy-start(bf16[3,2,192,128]{3,2,1,0:T(8,128)(2,1)} %copy-done.5) | copy-start | bytes 884740 | tf_op jit(solution)/shard_map/while
  90.0 2.2 %copy-start.8 = (bf16[3,2,192,128]{3,2,1,0:T(8,128)(2,1)S(1)}, bf16[3,2,192,128]{3,2,1,0:T(8,128)(2,1)}, u32[]{:S(2)}) copy-start(bf16[3,2,192,128]{3,2,1,0:T(8,128)(2,1)} %copy-done.7) | copy-start | bytes 884740 | tf_op jit(solution)/shard_map/while
  92.3 2.3 %copy-start = (bf16[4,192,192]{1,2,0:T(8,128)(2,1)}, bf16[4,192,192]{1,2,0:T(8,128)(2,1)S(1)}, u32[]{:S(2)}) copy-start(bf16[4,192,192]{1,2,0:T(8,128)(2,1)S(1)} %get-tuple-element.385) | copy-start | bytes 884740 | tf_op jit(solution)/shard_map/while
  92.3 2.3 %copy-start.3 = (bf16[3,2,192,128]{3,2,1,0:T(8,128)(2,1)}, bf16[3,2,192,128]{3,2,1,0:T(8,128)(2,1)S(1)}, u32[]{:S(2)}) copy-start(bf16[3,2,192,128]{3,2,1,0:T(8,128)(2,1)S(1)} %get-tuple-element.384) | copy-start | bytes 884740 | tf_op jit(solution)/shard_map/while
  92.3 2.3 %copy-start.5 = (bf16[3,2,192,128]{3,2,1,0:T(8,128)(2,1)}, bf16[3,2,192,128]{3,2,1,0:T(8,128)(2,1)S(1)}, u32[]{:S(2)}) copy-start(bf16[3,2,192,128]{3,2,1,0:T(8,128)(2,1)S(1)} %get-tuple-element.388) | copy-start | bytes 884740 | tf_op jit(solution)/shard_map/while
  92.3 2.3 %copy-start.7 = (bf16[3,2,192,128]{3,2,1,0:T(8,128)(2,1)}, bf16[3,2,192,128]{3,2,1,0:T(8,128)(2,1)S(1)}, u32[]{:S(2)}) copy-start(bf16[3,2,192,128]{3,2,1,0:T(8,128)(2,1)S(1)} %get-tuple-element.387) | copy-start | bytes 884740 | tf_op jit(solution)/shard_map/while
  95.5 0.9 copy-start.2
  97.9 2.2 %copy-start.1 = (bf16[4,192,192]{1,2,0:T(8,128)(2,1)S(1)}, bf16[4,192,192]{1,2,0:T(8,128)(2,1)}, u32[]{:S(2)}) copy-start(bf16[4,192,192]{1,2,0:T(8,128)(2,1)} %copy-done) | copy-start | bytes 884740 | tf_op jit(solution)/shard_map/while
  97.9 2.2 %copy-start.4 = (bf16[3,2,192,128]{3,2,1,0:T(8,128)(2,1)S(1)}, bf16[3,2,192,128]{3,2,1,0:T(8,128)(2,1)}, u32[]{:S(2)}) copy-start(bf16[3,2,192,128]{3,2,1,0:T(8,128)(2,1)} %copy-done.3) | copy-start | bytes 884740 | tf_op jit(solution)/shard_map/while
  97.9 2.2 %copy-start.6 = (bf16[3,2,192,128]{3,2,1,0:T(8,128)(2,1)S(1)}, bf16[3,2,192,128]{3,2,1,0:T(8,128)(2,1)}, u32[]{:S(2)}) copy-start(bf16[3,2,192,128]{3,2,1,0:T(8,128)(2,1)} %copy-done.5) | copy-start | bytes 884740 | tf_op jit(solution)/shard_map/while
  97.9 2.2 %copy-start.8 = (bf16[3,2,192,128]{3,2,1,0:T(8,128)(2,1)S(1)}, bf16[3,2,192,128]{3,2,1,0:T(8,128)(2,1)}, u32[]{:S(2)}) copy-start(bf16[3,2,192,128]{3,2,1,0:T(8,128)(2,1)} %copy-done.7) | copy-start | bytes 884740 | tf_op jit(solution)/shard_map/while
  100.1 2.3 %copy-start = (bf16[4,192,192]{1,2,0:T(8,128)(2,1)}, bf16[4,192,192]{1,2,0:T(8,128)(2,1)S(1)}, u32[]{:S(2)}) copy-start(bf16[4,192,192]{1,2,0:T(8,128)(2,1)S(1)} %get-tuple-element.385) | copy-start | bytes 884740 | tf_op jit(solution)/shard_map/while
  100.1 2.3 %copy-start.3 = (bf16[3,2,192,128]{3,2,1,0:T(8,128)(2,1)}, bf16[3,2,192,128]{3,2,1,0:T(8,128)(2,1)S(1)}, u32[]{:S(2)}) copy-start(bf16[3,2,192,128]{3,2,1,0:T(8,128)(2,1)S(1)} %get-tuple-element.384) | copy-start | bytes 884740 | tf_op jit(solution)/shard_map/while
  100.2 2.3 %copy-start.5 = (bf16[3,2,192,128]{3,2,1,0:T(8,128)(2,1)}, bf16[3,2,192,128]{3,2,1,0:T(8,128)(2,1)S(1)}, u32[]{:S(2)}) copy-start(bf16[3,2,192,128]{3,2,1,0:T(8,128)(2,1)S(1)} %get-tuple-element.388) | copy-start | bytes 884740 | tf_op jit(solution)/shard_map/while
  100.2 2.3 %copy-start.7 = (bf16[3,2,192,128]{3,2,1,0:T(8,128)(2,1)}, bf16[3,2,192,128]{3,2,1,0:T(8,128)(2,1)S(1)}, u32[]{:S(2)}) copy-start(bf16[3,2,192,128]{3,2,1,0:T(8,128)(2,1)S(1)} %get-tuple-element.387) | copy-start | bytes 884740 | tf_op jit(solution)/shard_map/while
  103.3 0.9 copy-start.2
  105.7 2.2 %copy-start.1 = (bf16[4,192,192]{1,2,0:T(8,128)(2,1)S(1)}, bf16[4,192,192]{1,2,0:T(8,128)(2,1)}, u32[]{:S(2)}) copy-start(bf16[4,192,192]{1,2,0:T(8,128)(2,1)} %copy-done) | copy-start | bytes 884740 | tf_op jit(solution)/shard_map/while
  105.7 2.2 %copy-start.4 = (bf16[3,2,192,128]{3,2,1,0:T(8,128)(2,1)S(1)}, bf16[3,2,192,128]{3,2,1,0:T(8,128)(2,1)}, u32[]{:S(2)}) copy-start(bf16[3,2,192,128]{3,2,1,0:T(8,128)(2,1)} %copy-done.3) | copy-start | bytes 884740 | tf_op jit(solution)/shard_map/while
  105.7 2.2 %copy-start.6 = (bf16[3,2,192,128]{3,2,1,0:T(8,128)(2,1)S(1)}, bf16[3,2,192,128]{3,2,1,0:T(8,128)(2,1)}, u32[]{:S(2)}) copy-start(bf16[3,2,192,128]{3,2,1,0:T(8,128)(2,1)} %copy-done.5) | copy-start | bytes 884740 | tf_op jit(solution)/shard_map/while
  105.7 2.2 %copy-start.8 = (bf16[3,2,192,128]{3,2,1,0:T(8,128)(2,1)S(1)}, bf16[3,2,192,128]{3,2,1,0:T(8,128)(2,1)}, u32[]{:S(2)}) copy-start(bf16[3,2,192,128]{3,2,1,0:T(8,128)(2,1)} %copy-done.7) | copy-start | bytes 884740 | tf_op jit(solution)/shard_map/while
  108.4 8.6 %copy-start.9 = (bf16[3,2,192,128]{3,2,1,0:T(8,128)(2,1)S(1)}, bf16[3,2,192,128]{3,2,1,0:T(8,128)(2,1)}, u32[]{:S(2)}) copy-start(bf16[3,2,192,128]{3,2,1,0:T(8,128)(2,1)} %get-tuple-element.144) | copy-start | bytes 884740
  111.6 23.8 %all-to-all-start.7 = ((bf16[6,192,128]{2,0,1:T(8,128)(2,1)}), bf16[6,192,128]{2,0,1:T(8,128)(2,1)S(1)}, u32[]{:S(2)}, u32[]{:S(2)}) async-start(bf16[6,192,128]{2,0,1:T(8,128)(2,1)} %copy.135), calls=%async_computation.7 | async-start | bytes 786432 | tf_op jit(solution)/shard_map/all_to_all | solution.py:125
  135.4 12.3 %all-to-all-start.5 = ((bf16[6,192,128]{2,0,1:T(8,128)(2,1)}), bf16[6,192,128]{2,0,1:T(8,128)(2,1)S(1)}, u32[]{:S(2)}, u32[]{:S(2)}) async-start(bf16[6,192,128]{2,0,1:T(8,128)(2,1)} %copy.127), calls=%async_computation.5 | async-start | bytes 786432 | tf_op jit(solution)/shard_map/all_to_all | solution.py:119
  147.7 12.3 %all-to-all-start.6 = ((bf16[6,192,128]{2,0,1:T(8,128)(2,1)}), bf16[6,192,128]{2,0,1:T(8,128)(2,1)S(1)}, u32[]{:S(2)}, u32[]{:S(2)}) async-start(bf16[6,192,128]{2,0,1:T(8,128)(2,1)} %copy.131), calls=%async_computation.6 | async-start | bytes 786432 | tf_op jit(solution)/shard_map/all_to_all | solution.py:122
  151.2 38.8 %reduce-scatter.5.cloned.1.call-start = ((), (), s32[]{:S(2)}) async-start(), calls=%async_computation.10 | async-start | bytes 442368 | tf_op jit(solution)/shard_map/reduce_scatter | solution.py:130
Sparse Core Ops, SparseCore 0:
  109.8 25.3 reduce-scatter.6
  155.6 34.3 reduce-scatter.4
